TPU v7x, 32 devices: a whole 2x2x4 slice. The times are simulated.
32 devices in a mesh: seq: 8 (over z, core), head: 4 (over y, x).
Axes of the slice: x: 2, y: 2, z: 4, core: 2. Of those that a mesh axis runs over, the one named last changes fastest.
Arguments:
- queries: bfloat16 [4096, 1024], P('seq', 'head'), may hold values from -6 to 6
- keys: bfloat16 [4096, 256], P(('seq', 'head')), may hold values from -6 to 6
- values: bfloat16 [4096, 256], P(('seq', 'head')), may hold values from -3 to 3
- attn_out: bfloat16 [4096, 1024], P('seq', 'head'), may hold values from -1.796875 to 1.796875
- out_grad: bfloat16 [4096, 1024], P('seq', 'head'), may hold values from -6 to 6
- log_norm: float32 [8, 4096], P('head', 'seq'), may hold values from 3.5 to 5.5
- block_layout: int32 [8, 32, 32], P('head'), may hold values 0 or 1
- document_ids: int32 [4096], replicated, may hold values from 0 to 7, never falling along the last dimension, each value on 1 to 2048 neighbouring positions
- block_order: int32 [32], replicated, may hold values from 0 to 31, each once
Outputs:
- query_grad: float32 [4096, 1024], P('seq', 'head')
- key_grad: float32 [4096, 256], P(('seq', 'head'))
- value_grad: float32 [4096, 256], P(('seq', 'head'))
Inputs may be any that keep to these rules, and one draw needn't show every extreme that they name: `document_ids`: never falls along the sequence position; each document covers 1 to 2048 positions, one exactly 2048. `block_order`: each sequence block once.
All inputs are finite; a program needn't handle non-finite values.
Results may differ from a plain program's by a relative error of at most 0.0029.
Values may be sent and summed in bfloat16 or wider, within the bound.
A program may use at most 128 MiB of HBM per device.

v0:
```python
import jax
import jax.numpy as jnp
from jax import lax
from jax.sharding import PartitionSpec as P

D_HEAD = 128
GROUP = 4
BLOCK = 128


def shifted(value, axis, steps):
    count = lax.axis_size(axis)
    pairs = [(source, (source + steps) % count) for source in range(count)]
    return lax.ppermute(value, axis, pairs)


def lookup_rows(first_row, count, block_order, document_ids):
    stored = first_row + jnp.arange(count, dtype=jnp.int32)
    blocks = stored // BLOCK
    table = jnp.arange(block_order.shape[0], dtype=jnp.int32)
    matches = blocks[:, None] == table[None, :]
    placed = jnp.sum(jnp.where(matches, block_order[None, :], 0), axis=1)
    position = placed * BLOCK + stored % BLOCK
    placed_hit = (placed[:, None] == table[None, :]).astype(jnp.float32)
    return (position, jnp.take(document_ids, position), placed_hit)


def body(
    queries, keys, values, attn_out, out_grad, log_norm, block_layout, document_ids, block_order
):
    tok_rows = queries.shape[0]
    head_count = log_norm.shape[0]
    head_width = D_HEAD
    kv_total = keys.shape[1] // head_width
    repeats = GROUP // head_count
    seq_size = lax.axis_size("seq")
    own_index = lax.axis_index("seq")
    scaling = head_width ** (-0.5)

    def widen(source):
        shaped = source.reshape(source.shape[0], kv_total, 1, head_width)
        shaped = jnp.broadcast_to(shaped, (source.shape[0], kv_total, repeats, head_width))
        return shaped.reshape(source.shape[0], kv_total * repeats * head_width)

    own_keys, own_values = (
        lax.all_to_all(widen(keys), "head", split_axis=1, concat_axis=0, tiled=True),
        lax.all_to_all(widen(values), "head", split_axis=1, concat_axis=0, tiled=True),
    )
    query_pos, query_docs, query_hit = lookup_rows(
        own_index * tok_rows, tok_rows, block_order, document_ids
    )
    query_heads = queries.reshape(tok_rows, head_count, head_width)
    grad_heads = out_grad.reshape(tok_rows, head_count, head_width)
    out_heads = attn_out.reshape(tok_rows, head_count, head_width)
    delta_rows = jnp.einsum(
        "qhd,qhd->hq", grad_heads, out_heads, preferred_element_type=jnp.float32
    )
    layout_rows = jnp.einsum("qa,hab->hqb", query_hit, block_layout.astype(jnp.float32))

    def block_grads(key_block, value_block, first_row):
        key_pos, key_docs, key_hit = lookup_rows(
            first_row, key_block.shape[0], block_order, document_ids
        )
        reach = jnp.einsum("hqb,kb->hqk", layout_rows, key_hit) > 0.5
        same_doc = (query_docs[:, None] == key_docs[None, :]) & (
            key_pos[None, :] <= query_pos[:, None]
        )
        reach = reach & same_doc[None, :, :]
        scores = (
            jnp.einsum("qhd,kd->hqk", query_heads, key_block, preferred_element_type=jnp.float32)
            * scaling
        )
        weights = jnp.where(reach, jnp.exp(scores - log_norm[:, :, None]), 0.0)
        weights_low = weights.astype(jnp.bfloat16)
        value_part = jnp.einsum(
            "hqk,qhd->kd", weights_low, grad_heads, preferred_element_type=jnp.float32
        )
        grad_scores = jnp.einsum(
            "qhd,kd->hqk", grad_heads, value_block, preferred_element_type=jnp.float32
        )
        score_grad = (weights * (grad_scores - delta_rows[:, :, None])).astype(jnp.bfloat16)
        query_part = jnp.einsum(
            "hqk,kd->qhd", score_grad, key_block, preferred_element_type=jnp.float32
        )
        key_part = jnp.einsum(
            "hqk,qhd->kd", score_grad, query_heads, preferred_element_type=jnp.float32
        )
        return (query_part, key_part, value_part)

    zero_query = jnp.zeros((tok_rows, head_count, head_width), jnp.float32)

    def pass_grads(totals):
        return shifted((totals[0], totals[1]), "seq", 1)

    def advance(turn_index, carried):
        key_block, value_block, key_total, value_total, query_total = carried
        source = (own_index - turn_index) % seq_size
        query_part, key_part, value_part = block_grads(key_block, value_block, source * tok_rows)
        key_block, value_block = shifted((key_block, value_block), "seq", 1)
        key_total, value_total = pass_grads((key_total + key_part, value_total + value_part))
        return (key_block, value_block, key_total, value_total, query_total + query_part)

    zero_key = jnp.zeros((tok_rows, head_width), jnp.float32)
    carried = lax.fori_loop(
        0, seq_size - 1, advance, (own_keys, own_values, zero_key, zero_key, zero_query)
    )
    key_block, value_block, key_total, value_total, query_total = carried
    source = (own_index - (seq_size - 1)) % seq_size
    query_part, key_part, value_part = block_grads(key_block, value_block, source * tok_rows)
    query_total = query_total + query_part
    key_total, value_total = pass_grads((key_total + key_part, value_total + value_part))
    key_scaled = key_total * scaling
    key_merged, value_merged = (
        lax.all_to_all(key_scaled, "head", split_axis=0, concat_axis=1, tiled=True),
        lax.all_to_all(value_total, "head", split_axis=0, concat_axis=1, tiled=True),
    )

    def fold_pairs(merged):
        row_count = merged.shape[0]
        return (
            merged.reshape(row_count, kv_total, repeats, head_width)
            .sum(axis=2)
            .reshape(row_count, kv_total * head_width)
        )

    query_grad = (query_total * scaling).reshape(tok_rows, head_count * head_width)
    return (query_grad, fold_pairs(key_merged), fold_pairs(value_merged))


def solution(mesh):
    in_specs = (
        P("seq", "head"),
        P(("seq", "head"), None),
        P(("seq", "head"), None),
        P("seq", "head"),
        P("seq", "head"),
        P("head", "seq"),
        P("head", None, None),
        P(),
        P(),
    )
    out_specs = (P("seq", "head"), P(("seq", "head"), None), P(("seq", "head"), None))
    return jax.shard_map(body, mesh=mesh, in_specs=in_specs, out_specs=out_specs, check_vma=False)
```

profile of v0, /device:TPU:0, one launch (start us, length us, event | category | flops | bytes accessed | tf_op | source)
XLA Modules:
  0.0 238.8 jit_solution(14379176686470545631)
XLA Ops:
  2.2 5.2 %all-to-all-start = ((bf16[128,4,128]{2,0,1:T(8,128)(2,1)}), bf16[128,4,128]{2,0,1:T(8,128)(2,1)}, u32[]{:S(2)}, u32[]{:S(2)}) async-start(bf16[128,4,128]{2,0,1:T(8,128)(2,1)} %bitcast.2), calls=%async_computation | async-start | bytes 262144 | tf_op jit(solution)/shard_map/all_to_all | solution.py:46
  12.9 3.1 %gather_fusion.1 = s32[512]{0:T(512)S(1)} fusion(s32[4096]{0:T(1024)S(1)} %copy-done.1, s32[1024]{0:T(1024)S(1)} %pad_clamp_fusion.2), kind=kCustom, calls=%fused_computation.1.clone | custom fusion | bytes 6144 | tf_op jit(solution)/shard_map/jit(_take)/gather | solution.py:25
  16.1 3.1 %gather_fusion.2 = s32[512]{0:T(512)S(1)} fusion(s32[4096]{0:T(1024)S(1)} %copy-done.1, s32[1024]{0:T(1024)S(1)} %pad_clamp_fusion.1), kind=kCustom, calls=%fused_computation.2.clone | custom fusion | bytes 6144 | tf_op jit(solution)/shard_map/jit(_take)/gather | solution.py:25
  20.5 1.7 compare_and_fusion.1
  24.1 4.2 %all-to-all-start.1 = ((bf16[128,4,128]{2,0,1:T(8,128)(2,1)}), bf16[128,4,128]{2,0,1:T(8,128)(2,1)}, u32[]{:S(2)}, u32[]{:S(2)}) async-start(bf16[128,4,128]{2,0,1:T(8,128)(2,1)} %bitcast.5), calls=%async_computation.1 | async-start | bytes 262144 | tf_op jit(solution)/shard_map/all_to_all | solution.py:47
  29.5 3.9 %all-to-all-done.1 = bf16[128,4,128]{2,0,1:T(8,128)(2,1)} async-done(((bf16[128,4,128]{2,0,1:T(8,128)(2,1)}), bf16[128,4,128]{2,0,1:T(8,128)(2,1)}, u32[]{:S(2)}, u32[]{:S(2)}) %all-to-all-start.1) | async-done | bytes 131104 | tf_op jit(solution)/shard_map/all_to_all | solution.py:47
  34.9 172.8 %while.25 = (s32[]{:T(128)}, bf16[512,128]{1,0:T(8,128)(2,1)}, bf16[512,128]{1,0:T(8,128)(2,1)}, f32[512,128]{1,0:T(8,128)}, f32[512,128]{1,0:T(8,128)}, /*index...) while((s32[]{:T(128)}, bf16[512,128]{1,0:T(8,128)(2,1)}, ...), condition=%wide.region_3.5_spmd.clone, body=%wide.region_1.4_spmd.clone.sunk | while | flops 710627840 | bytes 25690876 | solution.py:104
  36.7 1.9 collective-permute-start.1
  41.0 4.4 %gather_fusion = s32[512]{0:T(512)} fusion(s32[4096]{0:T(1024)S(1)} %get-tuple-element.762, s32[1024]{0:T(1024)} %pad_clamp_fusion.4), kind=kCustom, calls=%fused_computation.clone.clone.1 | custom fusion | bytes 6144 | tf_op jit(solution)/shard_map/while/body/eval_jaxpr/jit(_take)/gather | solution.py:25
  47.1 1.5 fusion.97
  50.6 1.7 collective-permute-start.3
  53.0 4.7 %collective-permute-done.2 = f32[512,128]{1,0:T(8,128)S(1)} collective-permute-done((f32[512,128]{1,0:T(8,128)S(1)}, f32[512,128]{1,0:T(8,128)S(1)}, u32[]{:S(2)}, u32[]{:S(2)}) %collective-permute-start.2) | collective-permute-done | bytes 262176 | tf_op jit(solution)/shard_map/while/body/eval_jaxpr/ppermute | solution.py:14
  57.7 2.8 %collective-permute-done.3 = f32[512,128]{1,0:T(8,128)S(1)} collective-permute-done((f32[512,128]{1,0:T(8,128)S(1)}, f32[512,128]{1,0:T(8,128)S(1)}, u32[]{:S(2)}, u32[]{:S(2)}) %collective-permute-start.3) | collective-permute-done | bytes 262176 | tf_op jit(solution)/shard_map/while/body/eval_jaxpr/ppermute | solution.py:14
  65.5 4.4 %gather_fusion = s32[512]{0:T(512)} fusion(s32[4096]{0:T(1024)S(1)} %get-tuple-element.762, s32[1024]{0:T(1024)} %pad_clamp_fusion.4), kind=kCustom, calls=%fused_computation.clone.clone.1 | custom fusion | bytes 6144 | tf_op jit(solution)/shard_map/while/body/eval_jaxpr/jit(_take)/gather | solution.py:25
  71.6 1.5 fusion.97
  75.0 1.6 collective-permute-start.3
  77.3 4.8 %collective-permute-done.2 = f32[512,128]{1,0:T(8,128)S(1)} collective-permute-done((f32[512,128]{1,0:T(8,128)S(1)}, f32[512,128]{1,0:T(8,128)S(1)}, u32[]{:S(2)}, u32[]{:S(2)}) %collective-permute-start.2) | collective-permute-done | bytes 262176 | tf_op jit(solution)/shard_map/while/body/eval_jaxpr/ppermute | solution.py:14
  82.1 2.8 %collective-permute-done.3 = f32[512,128]{1,0:T(8,128)S(1)} collective-permute-done((f32[512,128]{1,0:T(8,128)S(1)}, f32[512,128]{1,0:T(8,128)S(1)}, u32[]{:S(2)}, u32[]{:S(2)}) %collective-permute-start.3) | collective-permute-done | bytes 262176 | tf_op jit(solution)/shard_map/while/body/eval_jaxpr/ppermute | solution.py:14
  89.9 4.4 %gather_fusion = s32[512]{0:T(512)} fusion(s32[4096]{0:T(1024)S(1)} %get-tuple-element.762, s32[1024]{0:T(1024)} %pad_clamp_fusion.4), kind=kCustom, calls=%fused_computation.clone.clone.1 | custom fusion | bytes 6144 | tf_op jit(solution)/shard_map/while/body/eval_jaxpr/jit(_take)/gather | solution.py:25
  96.0 1.5 fusion.97
  100.1 6.4 %collective-permute-done.2 = f32[512,128]{1,0:T(8,128)S(1)} collective-permute-done((f32[512,128]{1,0:T(8,128)S(1)}, f32[512,128]{1,0:T(8,128)S(1)}, u32[]{:S(2)}, u32[]{:S(2)}) %collective-permute-start.2) | collective-permute-done | bytes 262176 | tf_op jit(solution)/shard_map/while/body/eval_jaxpr/ppermute | solution.py:14
  106.5 2.8 %collective-permute-done.3 = f32[512,128]{1,0:T(8,128)S(1)} collective-permute-done((f32[512,128]{1,0:T(8,128)S(1)}, f32[512,128]{1,0:T(8,128)S(1)}, u32[]{:S(2)}, u32[]{:S(2)}) %collective-permute-start.3) | collective-permute-done | bytes 262176 | tf_op jit(solution)/shard_map/while/body/eval_jaxpr/ppermute | solution.py:14
  114.3 4.4 %gather_fusion = s32[512]{0:T(512)} fusion(s32[4096]{0:T(1024)S(1)} %get-tuple-element.762, s32[1024]{0:T(1024)} %pad_clamp_fusion.4), kind=kCustom, calls=%fused_computation.clone.clone.1 | custom fusion | bytes 6144 | tf_op jit(solution)/shard_map/while/body/eval_jaxpr/jit(_take)/gather | solution.py:25
  120.4 1.5 fusion.97
  123.8 1.8 collective-permute-start.3
  126.3 4.6 %collective-permute-done.2 = f32[512,128]{1,0:T(8,128)S(1)} collective-permute-done((f32[512,128]{1,0:T(8,128)S(1)}, f32[512,128]{1,0:T(8,128)S(1)}, u32[]{:S(2)}, u32[]{:S(2)}) %collective-permute-start.2) | collective-permute-done | bytes 262176 | tf_op jit(solution)/shard_map/while/body/eval_jaxpr/ppermute | solution.py:14
  130.9 2.8 %collective-permute-done.3 = f32[512,128]{1,0:T(8,128)S(1)} collective-permute-done((f32[512,128]{1,0:T(8,128)S(1)}, f32[512,128]{1,0:T(8,128)S(1)}, u32[]{:S(2)}, u32[]{:S(2)}) %collective-permute-start.3) | collective-permute-done | bytes 262176 | tf_op jit(solution)/shard_map/while/body/eval_jaxpr/ppermute | solution.py:14
  138.7 4.4 %gather_fusion = s32[512]{0:T(512)} fusion(s32[4096]{0:T(1024)S(1)} %get-tuple-element.762, s32[1024]{0:T(1024)} %pad_clamp_fusion.4), kind=kCustom, calls=%fused_computation.clone.clone.1 | custom fusion | bytes 6144 | tf_op jit(solution)/shard_map/while/body/eval_jaxpr/jit(_take)/gather | solution.py:25
  144.8 1.5 fusion.97
  148.2 1.8 collective-permute-start.3
  150.7 4.6 %collective-permute-done.2 = f32[512,128]{1,0:T(8,128)S(1)} collective-permute-done((f32[512,128]{1,0:T(8,128)S(1)}, f32[512,128]{1,0:T(8,128)S(1)}, u32[]{:S(2)}, u32[]{:S(2)}) %collective-permute-start.2) | collective-permute-done | bytes 262176 | tf_op jit(solution)/shard_map/while/body/eval_jaxpr/ppermute | solution.py:14
  155.4 2.8 %collective-permute-done.3 = f32[512,128]{1,0:T(8,128)S(1)} collective-permute-done((f32[512,128]{1,0:T(8,128)S(1)}, f32[512,128]{1,0:T(8,128)S(1)}, u32[]{:S(2)}, u32[]{:S(2)}) %collective-permute-start.3) | collective-permute-done | bytes 262176 | tf_op jit(solution)/shard_map/while/body/eval_jaxpr/ppermute | solution.py:14
  163.1 4.4 %gather_fusion = s32[512]{0:T(512)} fusion(s32[4096]{0:T(1024)S(1)} %get-tuple-element.762, s32[1024]{0:T(1024)} %pad_clamp_fusion.4), kind=kCustom, calls=%fused_computation.clone.clone.1 | custom fusion | bytes 6144 | tf_op jit(solution)/shard_map/while/body/eval_jaxpr/jit(_take)/gather | solution.py:25
  169.2 1.5 fusion.97
  172.7 1.8 collective-permute-start.3
  175.2 4.6 %collective-permute-done.2 = f32[512,128]{1,0:T(8,128)S(1)} collective-permute-done((f32[512,128]{1,0:T(8,128)S(1)}, f32[512,128]{1,0:T(8,128)S(1)}, u32[]{:S(2)}, u32[]{:S(2)}) %collective-permute-start.2) | collective-permute-done | bytes 262176 | tf_op jit(solution)/shard_map/while/body/eval_jaxpr/ppermute | solution.py:14
  179.8 2.8 %collective-permute-done.3 = f32[512,128]{1,0:T(8,128)S(1)} collective-permute-done((f32[512,128]{1,0:T(8,128)S(1)}, f32[512,128]{1,0:T(8,128)S(1)}, u32[]{:S(2)}, u32[]{:S(2)}) %collective-permute-start.3) | collective-permute-done | bytes 262176 | tf_op jit(solution)/shard_map/while/body/eval_jaxpr/ppermute | solution.py:14
  187.6 4.4 %gather_fusion = s32[512]{0:T(512)} fusion(s32[4096]{0:T(1024)S(1)} %get-tuple-element.762, s32[1024]{0:T(1024)} %pad_clamp_fusion.4), kind=kCustom, calls=%fused_computation.clone.clone.1 | custom fusion | bytes 6144 | tf_op jit(solution)/shard_map/while/body/eval_jaxpr/jit(_take)/gather | solution.py:25
  193.7 1.5 fusion.97
  197.1 1.8 collective-permute-start.3
  199.6 4.6 %collective-permute-done.2 = f32[512,128]{1,0:T(8,128)S(1)} collective-permute-done((f32[512,128]{1,0:T(8,128)S(1)}, f32[512,128]{1,0:T(8,128)S(1)}, u32[]{:S(2)}, u32[]{:S(2)}) %collective-permute-start.2) | collective-permute-done | bytes 262176 | tf_op jit(solution)/shard_map/while/body/eval_jaxpr/ppermute | solution.py:14
  204.2 2.8 %collective-permute-done.3 = f32[512,128]{1,0:T(8,128)S(1)} collective-permute-done((f32[512,128]{1,0:T(8,128)S(1)}, f32[512,128]{1,0:T(8,128)S(1)}, u32[]{:S(2)}, u32[]{:S(2)}) %collective-permute-start.3) | collective-permute-done | bytes 262176 | tf_op jit(solution)/shard_map/while/body/eval_jaxpr/ppermute | solution.py:14
  207.8 2.2 fusion.22
  212.6 7.0 %collective-permute-done.4 = f32[512,128]{1,0:T(8,128)S(1)} collective-permute-done((f32[512,128]{1,0:T(8,128)S(1)}, f32[512,128]{1,0:T(8,128)S(1)}, u32[]{:S(2)}, u32[]{:S(2)}) %collective-permute-start.4) | collective-permute-done | bytes 262176 | tf_op jit(solution)/shard_map/ppermute | solution.py:14
  220.4 3.4 %all-to-all-start.2 = ((f32[4,128,128]{2,1,0:T(8,128)}), f32[4,128,128]{2,1,0:T(8,128)S(1)}, u32[]{:S(2)}, u32[]{:S(2)}) async-start(f32[4,128,128]{2,1,0:T(8,128)} %bitcast.26), calls=%async_computation.2 | async-start | bytes 524288 | tf_op jit(solution)/shard_map/all_to_all | solution.py:114
  224.0 5.1 %all-to-all-done.2 = f32[4,128,128]{2,1,0:T(8,128)S(1)} async-done(((f32[4,128,128]{2,1,0:T(8,128)}), f32[4,128,128]{2,1,0:T(8,128)S(1)}, u32[]{:S(2)}, u32[]{:S(2)}) %all-to-all-start.2) | async-done | bytes 262176 | tf_op jit(solution)/shard_map/all_to_all | solution.py:114
  229.2 3.4 %all-to-all-start.3 = ((f32[4,128,128]{2,1,0:T(8,128)}), f32[4,128,128]{2,1,0:T(8,128)S(1)}, u32[]{:S(2)}, u32[]{:S(2)}) async-start(f32[4,128,128]{2,1,0:T(8,128)} %bitcast.31), calls=%async_computation.3 | async-start | bytes 524288 | tf_op jit(solution)/shard_map/all_to_all | solution.py:115
  235.8 2.1 all-to-all-done.3
  (265 shorter events, 84.3 us)
Async XLA Ops:
  0.6 11.3 %copy-start.12 = (bf16[512,256]{1,0:T(8,128)(2,1)S(1)}, bf16[512,256]{1,0:T(8,128)(2,1)}, u32[]{:S(2)}) copy-start(bf16[512,256]{1,0:T(8,128)(2,1)} %param.17) | copy-start | bytes 786436
  0.7 12.1 %copy-start.13 = (bf16[512,256]{1,0:T(8,128)(2,1)S(1)}, bf16[512,256]{1,0:T(8,128)(2,1)}, u32[]{:S(2)}) copy-start(bf16[512,256]{1,0:T(8,128)(2,1)} %param.16) | copy-start | bytes 786436
  2.2 21.3 %all-to-all-start = ((bf16[128,4,128]{2,0,1:T(8,128)(2,1)}), bf16[128,4,128]{2,0,1:T(8,128)(2,1)}, u32[]{:S(2)}, u32[]{:S(2)}) async-start(bf16[128,4,128]{2,0,1:T(8,128)(2,1)} %bitcast.2), calls=%async_computation | async-start | bytes 262144 | tf_op jit(solution)/shard_map/all_to_all | solution.py:46
  7.3 5.6 %copy-start.1 = (s32[4096]{0:T(1024)S(1)}, s32[4096]{0:T(1024)}, u32[]{:S(2)}) copy-start(s32[4096]{0:T(1024)} %param.20) | copy-start | bytes 49156
  12.4 6.8 %copy-start.8 = (bf16[512,256]{0,1:T(8,128)(2,1)}, bf16[512,256]{0,1:T(8,128)(2,1)S(1)}, u32[]{:S(2)}) copy-start(bf16[512,256]{0,1:T(8,128)(2,1)S(1)} %copy.89) | copy-start | bytes 786436
  24.1 9.3 %all-to-all-start.1 = ((bf16[128,4,128]{2,0,1:T(8,128)(2,1)}), bf16[128,4,128]{2,0,1:T(8,128)(2,1)}, u32[]{:S(2)}, u32[]{:S(2)}) async-start(bf16[128,4,128]{2,0,1:T(8,128)(2,1)} %bitcast.5), calls=%async_computation.1 | async-start | bytes 262144 | tf_op jit(solution)/shard_map/all_to_all | solution.py:47
  35.8 17.1 %collective-permute-start = (bf16[512,128]{1,0:T(8,128)(2,1)S(1)}, bf16[512,128]{1,0:T(8,128)(2,1)}, u32[]{:S(2)}, u32[]{:S(2)}) collective-permute-start(bf16[512,128]{1,0:T(8,128)(2,1)S(1)} %copy.137), channel_id=1, source_target_pairs={{0,4},{4,8},{8,12},{12,16},{16,20},{20,24},{24,28},{28,0},{1,5},{5... | collective-permute-start | bytes 393224 | tf_op jit(solution)/shard_map/while/body/eval_jaxpr/ppermute | solution.py:14
  36.7 16.2 %collective-permute-start.1 = (bf16[512,128]{1,0:T(8,128)(2,1)S(1)}, bf16[512,128]{1,0:T(8,128)(2,1)}, u32[]{:S(2)}, u32[]{:S(2)}) collective-permute-start(bf16[512,128]{1,0:T(8,128)(2,1)S(1)} %copy.138), channel_id=1, source_target_pairs={{0,4},{4,8},{8,12},{12,16},{16,20},{20,24},{24,28},{28,0},{1,5},{5... | collective-permute-start | bytes 393224 | tf_op jit(solution)/shard_map/while/body/eval_jaxpr/ppermute | solution.py:14
  50.0 7.6 %collective-permute-start.2 = (f32[512,128]{1,0:T(8,128)S(1)}, f32[512,128]{1,0:T(8,128)S(1)}, u32[]{:S(2)}, u32[]{:S(2)}) collective-permute-start(f32[512,128]{1,0:T(8,128)S(1)} %fusion.99), channel_id=1, source_target_pairs={{0,4},{4,8},{8,12},{12,16},{16,20},{20,24},{24,28},{28,0},{1,5},{5... | collective-permute-start | bytes 786440 | tf_op jit(solution)/shard_map/while/body/eval_jaxpr/ppermute | solution.py:14
  50.6 9.9 %collective-permute-start.3 = (f32[512,128]{1,0:T(8,128)S(1)}, f32[512,128]{1,0:T(8,128)S(1)}, u32[]{:S(2)}, u32[]{:S(2)}) collective-permute-start(f32[512,128]{1,0:T(8,128)S(1)} %fusion.100), channel_id=1, source_target_pairs={{0,4},{4,8},{8,12},{12,16},{16,20},{20,24},{24,28},{28,0},{1,5},{5... | collective-permute-start | bytes 786440 | tf_op jit(solution)/shard_map/while/body/eval_jaxpr/ppermute | solution.py:14
  57.7 2.8 %copy-start.3 = (f32[512,128]{1,0:T(8,128)}, f32[512,128]{1,0:T(8,128)S(1)}, u32[]{:S(2)}) copy-start(f32[512,128]{1,0:T(8,128)S(1)} %collective-permute-done.2) | copy-start | bytes 786436 | tf_op jit(solution)/shard_map/while
  62.1 15.1 %collective-permute-start = (bf16[512,128]{1,0:T(8,128)(2,1)S(1)}, bf16[512,128]{1,0:T(8,128)(2,1)}, u32[]{:S(2)}, u32[]{:S(2)}) collective-permute-start(bf16[512,128]{1,0:T(8,128)(2,1)S(1)} %copy.137), channel_id=1, source_target_pairs={{0,4},{4,8},{8,12},{12,16},{16,20},{20,24},{24,28},{28,0},{1,5},{5... | collective-permute-start | bytes 393224 | tf_op jit(solution)/shard_map/while/body/eval_jaxpr/ppermute | solution.py:14
  63.0 14.2 %collective-permute-start.1 = (bf16[512,128]{1,0:T(8,128)(2,1)S(1)}, bf16[512,128]{1,0:T(8,128)(2,1)}, u32[]{:S(2)}, u32[]{:S(2)}) collective-permute-start(bf16[512,128]{1,0:T(8,128)(2,1)S(1)} %copy.138), channel_id=1, source_target_pairs={{0,4},{4,8},{8,12},{12,16},{16,20},{20,24},{24,28},{28,0},{1,5},{5... | collective-permute-start | bytes 393224 | tf_op jit(solution)/shard_map/while/body/eval_jaxpr/ppermute | solution.py:14
  74.5 7.7 %collective-permute-start.2 = (f32[512,128]{1,0:T(8,128)S(1)}, f32[512,128]{1,0:T(8,128)S(1)}, u32[]{:S(2)}, u32[]{:S(2)}) collective-permute-start(f32[512,128]{1,0:T(8,128)S(1)} %fusion.99), channel_id=1, source_target_pairs={{0,4},{4,8},{8,12},{12,16},{16,20},{20,24},{24,28},{28,0},{1,5},{5... | collective-permute-start | bytes 786440 | tf_op jit(solution)/shard_map/while/body/eval_jaxpr/ppermute | solution.py:14
  75.0 9.9 %collective-permute-start.3 = (f32[512,128]{1,0:T(8,128)S(1)}, f32[512,128]{1,0:T(8,128)S(1)}, u32[]{:S(2)}, u32[]{:S(2)}) collective-permute-start(f32[512,128]{1,0:T(8,128)S(1)} %fusion.100), channel_id=1, source_target_pairs={{0,4},{4,8},{8,12},{12,16},{16,20},{20,24},{24,28},{28,0},{1,5},{5... | collective-permute-start | bytes 786440 | tf_op jit(solution)/shard_map/while/body/eval_jaxpr/ppermute | solution.py:14
  82.1 2.8 %copy-start.3 = (f32[512,128]{1,0:T(8,128)}, f32[512,128]{1,0:T(8,128)S(1)}, u32[]{:S(2)}) copy-start(f32[512,128]{1,0:T(8,128)S(1)} %collective-permute-done.2) | copy-start | bytes 786436 | tf_op jit(solution)/shard_map/while
  86.5 13.6 %collective-permute-start = (bf16[512,128]{1,0:T(8,128)(2,1)S(1)}, bf16[512,128]{1,0:T(8,128)(2,1)}, u32[]{:S(2)}, u32[]{:S(2)}) collective-permute-start(bf16[512,128]{1,0:T(8,128)(2,1)S(1)} %copy.137), channel_id=1, source_target_pairs={{0,4},{4,8},{8,12},{12,16},{16,20},{20,24},{24,28},{28,0},{1,5},{5... | collective-permute-start | bytes 393224 | tf_op jit(solution)/shard_map/while/body/eval_jaxpr/ppermute | solution.py:14
  87.5 12.7 %collective-permute-start.1 = (bf16[512,128]{1,0:T(8,128)(2,1)S(1)}, bf16[512,128]{1,0:T(8,128)(2,1)}, u32[]{:S(2)}, u32[]{:S(2)}) collective-permute-start(bf16[512,128]{1,0:T(8,128)(2,1)S(1)} %copy.138), channel_id=1, source_target_pairs={{0,4},{4,8},{8,12},{12,16},{16,20},{20,24},{24,28},{28,0},{1,5},{5... | collective-permute-start | bytes 393224 | tf_op jit(solution)/shard_map/while/body/eval_jaxpr/ppermute | solution.py:14
  98.9 7.7 %collective-permute-start.2 = (f32[512,128]{1,0:T(8,128)S(1)}, f32[512,128]{1,0:T(8,128)S(1)}, u32[]{:S(2)}, u32[]{:S(2)}) collective-permute-start(f32[512,128]{1,0:T(8,128)S(1)} %fusion.99), channel_id=1, source_target_pairs={{0,4},{4,8},{8,12},{12,16},{16,20},{20,24},{24,28},{28,0},{1,5},{5... | collective-permute-start | bytes 786440 | tf_op jit(solution)/shard_map/while/body/eval_jaxpr/ppermute | solution.py:14
  99.4 9.9 %collective-permute-start.3 = (f32[512,128]{1,0:T(8,128)S(1)}, f32[512,128]{1,0:T(8,128)S(1)}, u32[]{:S(2)}, u32[]{:S(2)}) collective-permute-start(f32[512,128]{1,0:T(8,128)S(1)} %fusion.100), channel_id=1, source_target_pairs={{0,4},{4,8},{8,12},{12,16},{16,20},{20,24},{24,28},{28,0},{1,5},{5... | collective-permute-start | bytes 786440 | tf_op jit(solution)/shard_map/while/body/eval_jaxpr/ppermute | solution.py:14
  106.5 2.8 %copy-start.3 = (f32[512,128]{1,0:T(8,128)}, f32[512,128]{1,0:T(8,128)S(1)}, u32[]{:S(2)}) copy-start(f32[512,128]{1,0:T(8,128)S(1)} %collective-permute-done.2) | copy-start | bytes 786436 | tf_op jit(solution)/shard_map/while
  111.0 15.3 %collective-permute-start = (bf16[512,128]{1,0:T(8,128)(2,1)S(1)}, bf16[512,128]{1,0:T(8,128)(2,1)}, u32[]{:S(2)}, u32[]{:S(2)}) collective-permute-start(bf16[512,128]{1,0:T(8,128)(2,1)S(1)} %copy.137), channel_id=1, source_target_pairs={{0,4},{4,8},{8,12},{12,16},{16,20},{20,24},{24,28},{28,0},{1,5},{5... | collective-permute-start | bytes 393224 | tf_op jit(solution)/shard_map/while/body/eval_jaxpr/ppermute | solution.py:14
  111.9 14.4 %collective-permute-start.1 = (bf16[512,128]{1,0:T(8,128)(2,1)S(1)}, bf16[512,128]{1,0:T(8,128)(2,1)}, u32[]{:S(2)}, u32[]{:S(2)}) collective-permute-start(bf16[512,128]{1,0:T(8,128)(2,1)S(1)} %copy.138), channel_id=1, source_target_pairs={{0,4},{4,8},{8,12},{12,16},{16,20},{20,24},{24,28},{28,0},{1,5},{5... | collective-permute-start | bytes 393224 | tf_op jit(solution)/shard_map/while/body/eval_jaxpr/ppermute | solution.py:14
  123.3 7.7 %collective-permute-start.2 = (f32[512,128]{1,0:T(8,128)S(1)}, f32[512,128]{1,0:T(8,128)S(1)}, u32[]{:S(2)}, u32[]{:S(2)}) collective-permute-start(f32[512,128]{1,0:T(8,128)S(1)} %fusion.99), channel_id=1, source_target_pairs={{0,4},{4,8},{8,12},{12,16},{16,20},{20,24},{24,28},{28,0},{1,5},{5... | collective-permute-start | bytes 786440 | tf_op jit(solution)/shard_map/while/body/eval_jaxpr/ppermute | solution.py:14
  123.8 9.9 %collective-permute-start.3 = (f32[512,128]{1,0:T(8,128)S(1)}, f32[512,128]{1,0:T(8,128)S(1)}, u32[]{:S(2)}, u32[]{:S(2)}) collective-permute-start(f32[512,128]{1,0:T(8,128)S(1)} %fusion.100), channel_id=1, source_target_pairs={{0,4},{4,8},{8,12},{12,16},{16,20},{20,24},{24,28},{28,0},{1,5},{5... | collective-permute-start | bytes 786440 | tf_op jit(solution)/shard_map/while/body/eval_jaxpr/ppermute | solution.py:14
  130.9 2.8 %copy-start.3 = (f32[512,128]{1,0:T(8,128)}, f32[512,128]{1,0:T(8,128)S(1)}, u32[]{:S(2)}) copy-start(f32[512,128]{1,0:T(8,128)S(1)} %collective-permute-done.2) | copy-start | bytes 786436 | tf_op jit(solution)/shard_map/while
  135.4 15.3 %collective-permute-start = (bf16[512,128]{1,0:T(8,128)(2,1)S(1)}, bf16[512,128]{1,0:T(8,128)(2,1)}, u32[]{:S(2)}, u32[]{:S(2)}) collective-permute-start(bf16[512,128]{1,0:T(8,128)(2,1)S(1)} %copy.137), channel_id=1, source_target_pairs={{0,4},{4,8},{8,12},{12,16},{16,20},{20,24},{24,28},{28,0},{1,5},{5... | collective-permute-start | bytes 393224 | tf_op jit(solution)/shard_map/while/body/eval_jaxpr/ppermute | solution.py:14
  136.3 14.4 %collective-permute-start.1 = (bf16[512,128]{1,0:T(8,128)(2,1)S(1)}, bf16[512,128]{1,0:T(8,128)(2,1)}, u32[]{:S(2)}, u32[]{:S(2)}) collective-permute-start(bf16[512,128]{1,0:T(8,128)(2,1)S(1)} %copy.138), channel_id=1, source_target_pairs={{0,4},{4,8},{8,12},{12,16},{16,20},{20,24},{24,28},{28,0},{1,5},{5... | collective-permute-start | bytes 393224 | tf_op jit(solution)/shard_map/while/body/eval_jaxpr/ppermute | solution.py:14
  147.7 7.7 %collective-permute-start.2 = (f32[512,128]{1,0:T(8,128)S(1)}, f32[512,128]{1,0:T(8,128)S(1)}, u32[]{:S(2)}, u32[]{:S(2)}) collective-permute-start(f32[512,128]{1,0:T(8,128)S(1)} %fusion.99), channel_id=1, source_target_pairs={{0,4},{4,8},{8,12},{12,16},{16,20},{20,24},{24,28},{28,0},{1,5},{5... | collective-permute-start | bytes 786440 | tf_op jit(solution)/shard_map/while/body/eval_jaxpr/ppermute | solution.py:14
  148.2 9.9 %collective-permute-start.3 = (f32[512,128]{1,0:T(8,128)S(1)}, f32[512,128]{1,0:T(8,128)S(1)}, u32[]{:S(2)}, u32[]{:S(2)}) collective-permute-start(f32[512,128]{1,0:T(8,128)S(1)} %fusion.100), channel_id=1, source_target_pairs={{0,4},{4,8},{8,12},{12,16},{16,20},{20,24},{24,28},{28,0},{1,5},{5... | collective-permute-start | bytes 786440 | tf_op jit(solution)/shard_map/while/body/eval_jaxpr/ppermute | solution.py:14
  155.4 2.8 %copy-start.3 = (f32[512,128]{1,0:T(8,128)}, f32[512,128]{1,0:T(8,128)S(1)}, u32[]{:S(2)}) copy-start(f32[512,128]{1,0:T(8,128)S(1)} %collective-permute-done.2) | copy-start | bytes 786436 | tf_op jit(solution)/shard_map/while
  159.8 15.3 %collective-permute-start = (bf16[512,128]{1,0:T(8,128)(2,1)S(1)}, bf16[512,128]{1,0:T(8,128)(2,1)}, u32[]{:S(2)}, u32[]{:S(2)}) collective-permute-start(bf16[512,128]{1,0:T(8,128)(2,1)S(1)} %copy.137), channel_id=1, source_target_pairs={{0,4},{4,8},{8,12},{12,16},{16,20},{20,24},{24,28},{28,0},{1,5},{5... | collective-permute-start | bytes 393224 | tf_op jit(solution)/shard_map/while/body/eval_jaxpr/ppermute | solution.py:14
  160.7 14.4 %collective-permute-start.1 = (bf16[512,128]{1,0:T(8,128)(2,1)S(1)}, bf16[512,128]{1,0:T(8,128)(2,1)}, u32[]{:S(2)}, u32[]{:S(2)}) collective-permute-start(bf16[512,128]{1,0:T(8,128)(2,1)S(1)} %copy.138), channel_id=1, source_target_pairs={{0,4},{4,8},{8,12},{12,16},{16,20},{20,24},{24,28},{28,0},{1,5},{5... | collective-permute-start | bytes 393224 | tf_op jit(solution)/shard_map/while/body/eval_jaxpr/ppermute | solution.py:14
  172.1 7.7 %collective-permute-start.2 = (f32[512,128]{1,0:T(8,128)S(1)}, f32[512,128]{1,0:T(8,128)S(1)}, u32[]{:S(2)}, u32[]{:S(2)}) collective-permute-start(f32[512,128]{1,0:T(8,128)S(1)} %fusion.99), channel_id=1, source_target_pairs={{0,4},{4,8},{8,12},{12,16},{16,20},{20,24},{24,28},{28,0},{1,5},{5... | collective-permute-start | bytes 786440 | tf_op jit(solution)/shard_map/while/body/eval_jaxpr/ppermute | solution.py:14
  172.7 9.9 %collective-permute-start.3 = (f32[512,128]{1,0:T(8,128)S(1)}, f32[512,128]{1,0:T(8,128)S(1)}, u32[]{:S(2)}, u32[]{:S(2)}) collective-permute-start(f32[512,128]{1,0:T(8,128)S(1)} %fusion.100), channel_id=1, source_target_pairs={{0,4},{4,8},{8,12},{12,16},{16,20},{20,24},{24,28},{28,0},{1,5},{5... | collective-permute-start | bytes 786440 | tf_op jit(solution)/shard_map/while/body/eval_jaxpr/ppermute | solution.py:14
  179.8 2.8 %copy-start.3 = (f32[512,128]{1,0:T(8,128)}, f32[512,128]{1,0:T(8,128)S(1)}, u32[]{:S(2)}) copy-start(f32[512,128]{1,0:T(8,128)S(1)} %collective-permute-done.2) | copy-start | bytes 786436 | tf_op jit(solution)/shard_map/while
  184.2 15.3 %collective-permute-start = (bf16[512,128]{1,0:T(8,128)(2,1)S(1)}, bf16[512,128]{1,0:T(8,128)(2,1)}, u32[]{:S(2)}, u32[]{:S(2)}) collective-permute-start(bf16[512,128]{1,0:T(8,128)(2,1)S(1)} %copy.137), channel_id=1, source_target_pairs={{0,4},{4,8},{8,12},{12,16},{16,20},{20,24},{24,28},{28,0},{1,5},{5... | collective-permute-start | bytes 393224 | tf_op jit(solution)/shard_map/while/body/eval_jaxpr/ppermute | solution.py:14
  185.1 14.4 %collective-permute-start.1 = (bf16[512,128]{1,0:T(8,128)(2,1)S(1)}, bf16[512,128]{1,0:T(8,128)(2,1)}, u32[]{:S(2)}, u32[]{:S(2)}) collective-permute-start(bf16[512,128]{1,0:T(8,128)(2,1)S(1)} %copy.138), channel_id=1, source_target_pairs={{0,4},{4,8},{8,12},{12,16},{16,20},{20,24},{24,28},{28,0},{1,5},{5... | collective-permute-start | bytes 393224 | tf_op jit(solution)/shard_map/while/body/eval_jaxpr/ppermute | solution.py:14
  196.6 7.7 %collective-permute-start.2 = (f32[512,128]{1,0:T(8,128)S(1)}, f32[512,128]{1,0:T(8,128)S(1)}, u32[]{:S(2)}, u32[]{:S(2)}) collective-permute-start(f32[512,128]{1,0:T(8,128)S(1)} %fusion.99), channel_id=1, source_target_pairs={{0,4},{4,8},{8,12},{12,16},{16,20},{20,24},{24,28},{28,0},{1,5},{5... | collective-permute-start | bytes 786440 | tf_op jit(solution)/shard_map/while/body/eval_jaxpr/ppermute | solution.py:14
  197.1 9.9 %collective-permute-start.3 = (f32[512,128]{1,0:T(8,128)S(1)}, f32[512,128]{1,0:T(8,128)S(1)}, u32[]{:S(2)}, u32[]{:S(2)}) collective-permute-start(f32[512,128]{1,0:T(8,128)S(1)} %fusion.100), channel_id=1, source_target_pairs={{0,4},{4,8},{8,12},{12,16},{16,20},{20,24},{24,28},{28,0},{1,5},{5... | collective-permute-start | bytes 786440 | tf_op jit(solution)/shard_map/while/body/eval_jaxpr/ppermute | solution.py:14
  204.2 2.8 %copy-start.3 = (f32[512,128]{1,0:T(8,128)}, f32[512,128]{1,0:T(8,128)S(1)}, u32[]{:S(2)}) copy-start(f32[512,128]{1,0:T(8,128)S(1)} %collective-permute-done.2) | copy-start | bytes 786436 | tf_op jit(solution)/shard_map/while
  207.7 2.3 copy-start.9
  207.7 2.3 copy-start.15
  210.0 2.1 copy-start.7
  212.0 7.6 %collective-permute-start.4 = (f32[512,128]{1,0:T(8,128)S(1)}, f32[512,128]{1,0:T(8,128)S(1)}, u32[]{:S(2)}, u32[]{:S(2)}) collective-permute-start(f32[512,128]{1,0:T(8,128)S(1)} %fusion.27), channel_id=1, source_target_pairs={{0,4},{4,8},{8,12},{12,16},{16,20},{20,24},{24,28},{28,0},{1,5},{5... | collective-permute-start | bytes 786440 | tf_op jit(solution)/shard_map/ppermute | solution.py:14
  212.6 11.4 %collective-permute-start.5 = (f32[512,128]{1,0:T(8,128)S(1)}, f32[512,128]{1,0:T(8,128)}, u32[]{:S(2)}, u32[]{:S(2)}) collective-permute-start(f32[512,128]{1,0:T(8,128)S(1)} %fusion.28), channel_id=1, source_target_pairs={{0,4},{4,8},{8,12},{12,16},{16,20},{20,24},{24,28},{28,0},{1,5},{5... | collective-permute-start | bytes 786440 | tf_op jit(solution)/shard_map/ppermute | solution.py:14
  220.4 8.8 %all-to-all-start.2 = ((f32[4,128,128]{2,1,0:T(8,128)}), f32[4,128,128]{2,1,0:T(8,128)S(1)}, u32[]{:S(2)}, u32[]{:S(2)}) async-start(f32[4,128,128]{2,1,0:T(8,128)} %bitcast.26), calls=%async_computation.2 | async-start | bytes 524288 | tf_op jit(solution)/shard_map/all_to_all | solution.py:114
  229.2 8.8 %all-to-all-start.3 = ((f32[4,128,128]{2,1,0:T(8,128)}), f32[4,128,128]{2,1,0:T(8,128)S(1)}, u32[]{:S(2)}, u32[]{:S(2)}) async-start(f32[4,128,128]{2,1,0:T(8,128)} %bitcast.31), calls=%async_computation.3 | async-start | bytes 524288 | tf_op jit(solution)/shard_map/all_to_all | solution.py:115
  (33 other events, 37.7 us)
where the time goes:
time: 241 us; the launch traced here: 239 us
  waiting for transfers between devices  72.3 us (30%)
  local copies, waits for them, and re-layouts  69.5 us (29%)
  matrix products  34.9 us (14%)
  other arithmetic  30.9 us (13%)
  starting transfers between devices  29.3 us (12%)
    ppermute x30, waiting for transfers between devices, shifted(): return lax.ppermute(value, axis, pairs)  61.2 us
    gather x9, local copies, waits for them, and re-layouts, lookup_rows(): return (position, jnp.take(document_ids, position), placed_hit)  37.3 us
    while x84, local copies, waits for them, and re-layouts  21.2 us
    ppermute x30, starting transfers between devices, shifted(): return lax.ppermute(value, axis, pairs)  13.1 us
    dot_general x8, matrix products, block_grads(): jnp.einsum('qhd,kd->hqk', query_heads, key_block, preferred_element_type=...  12.6 us
    select_n x18, other arithmetic, lookup_rows(): return (position, jnp.take(document_ids, position), placed_hit)  10.2 us
    and x8, other arithmetic, block_grads(): (query_docs[:, None] == key_docs[None, :]) & (key_pos[None, :] <= query_p...  8.32 us
    unnamed x32, local copies, waits for them, and re-layouts  6.05 us
  transfers between devices with their start and end apart: 34, of which 18 were waited for; matrix products, arithmetic and copies ran while one was open for 46% of the time, Pallas kernels for 0%

commit v1 on v0

v1 whole, which is shorter than its diff:
```python
import functools
import math

import jax
import jax.numpy as jnp
from jax import lax
from jax.experimental import pallas as pl
from jax.experimental.pallas import tpu as pltpu
from jax.sharding import PartitionSpec as P

D_HEAD = 128
GROUP = 4
BLOCK = 128
DOCS = 8
CHUNK = 4
LOG2E = math.log2(math.e)
NT = (((1,), (1,)), ((), ()))
TN = (((0,), (0,)), ((), ()))


def grads_kernel(
    order, first, starts, layout, docs, q_ref, do_ref, o_ref, ln_ref, kv_ref,
    dq_ref, dkv_ref, acc, inverse, dqt,
):
    heads = ln_ref.shape[0]
    blocks = order.shape[0]
    own = q_ref.shape[0] // BLOCK
    scale = D_HEAD ** -0.5
    me = lax.axis_index("seq")
    wide = heads * BLOCK

    def clear(r, _):
        inverse[order[r]] = r
        acc[pl.ds(r * BLOCK, BLOCK), :] = jnp.zeros((BLOCK, 2 * D_HEAD), jnp.float32)
        return 0

    lax.fori_loop(0, blocks, clear, 0)
    lane = lax.broadcasted_iota(jnp.int32, (1, wide), 1)
    sub = lax.broadcasted_iota(jnp.int32, (BLOCK, wide), 0)

    def per_query_block(i, _):
        rows = pl.ds(i * BLOCK, BLOCK)
        qb = order[me * own + i]
        ids = docs[pl.ds(qb, 1), :]
        low = jnp.zeros((1, BLOCK), jnp.int32)
        for d in range(1, DOCS):
            low = jnp.where(ids >= d, starts[d], low)
        low = jnp.concatenate([low] * heads, axis=1)
        high = qb * BLOCK + lane % BLOCK
        q2 = jnp.concatenate(
            [q_ref[rows, h * D_HEAD:(h + 1) * D_HEAD] for h in range(heads)], axis=0)
        do2 = jnp.concatenate(
            [do_ref[rows, h * D_HEAD:(h + 1) * D_HEAD] for h in range(heads)], axis=0)
        o2 = jnp.concatenate(
            [o_ref[rows, h * D_HEAD:(h + 1) * D_HEAD] for h in range(heads)], axis=0)
        product = do2.astype(jnp.float32) * o2.astype(jnp.float32)
        delta = jnp.sum(product.T, axis=0, keepdims=True)
        norm = jnp.concatenate([ln_ref[h:h + 1, rows] for h in range(heads)], axis=1) * LOG2E
        dqt[...] = jnp.zeros_like(dqt)
        begin = first[qb]
        trips = (qb - begin + CHUNK) // CHUNK

        def per_chunk(t, _):
            slots, keeps, ks, vs = [], [], [], []
            for c in range(CHUNK):
                kb = begin + t * CHUNK + c
                held = jnp.minimum(kb, qb)
                slot = pl.multiple_of(inverse[held] * BLOCK, BLOCK)
                slots.append(slot)
                top = jnp.full((1, wide), -1, jnp.int32)
                for h in range(heads):
                    on = (layout[(h * blocks + qb) * blocks + held] == 1) & (kb <= qb)
                    limit = jnp.where(on, 1 << 30, -1)
                    top = jnp.where(lane // BLOCK == h, jnp.minimum(high, limit), top)
                keeps.append((sub >= low - held * BLOCK) & (sub <= top - held * BLOCK))
                ks.append(kv_ref[pl.ds(slot, BLOCK), :D_HEAD])
                vs.append(kv_ref[pl.ds(slot, BLOCK), D_HEAD:])
            k4 = jnp.concatenate(ks, axis=0)
            v4 = jnp.concatenate(vs, axis=0)
            keep = jnp.concatenate(keeps, axis=0)
            st = lax.dot_general(k4, q2, NT, preferred_element_type=jnp.float32)
            dpt = lax.dot_general(v4, do2, NT, preferred_element_type=jnp.float32)
            w = jnp.where(keep, jnp.exp2(st * (scale * LOG2E) - norm), 0.0)
            wl = w.astype(jnp.bfloat16)
            dv = jnp.dot(wl, do2, preferred_element_type=jnp.float32)
            ds = (w * (dpt - delta)).astype(jnp.bfloat16)
            dk = jnp.dot(ds, q2, preferred_element_type=jnp.float32)
            dqt[...] += lax.dot_general(k4, ds, TN, preferred_element_type=jnp.float32)
            for c in range(CHUNK):
                part = slice(c * BLOCK, (c + 1) * BLOCK)
                acc[pl.ds(slots[c], BLOCK), :D_HEAD] += dk[part]
                acc[pl.ds(slots[c], BLOCK), D_HEAD:] += dv[part]
            return 0

        lax.fori_loop(0, trips, per_chunk, 0)
        for h in range(heads):
            dq_ref[rows, h * D_HEAD:(h + 1) * D_HEAD] = (
                dqt[:, h * BLOCK:(h + 1) * BLOCK].T * scale)
        return 0

    lax.fori_loop(0, own, per_query_block, 0)

    def finish(r, _):
        rows = pl.ds(r * BLOCK, BLOCK)
        dkv_ref[rows, :D_HEAD] = (acc[rows, :D_HEAD] * scale).astype(dkv_ref.dtype)
        dkv_ref[rows, D_HEAD:] = acc[rows, D_HEAD:].astype(dkv_ref.dtype)
        return 0

    lax.fori_loop(0, blocks, finish, 0)


def local_grads(queries, out_grad, attn_out, log_norm, kv_all, block_layout, document_ids,
                block_order, sum_type):
    blocks = block_order.shape[0]
    total = kv_all.shape[0]
    starts = jnp.sum(
        (document_ids[None, :] < jnp.arange(DOCS, dtype=jnp.int32)[:, None]).astype(jnp.int32),
        axis=1)
    heads_of = document_ids.reshape(blocks, BLOCK)
    first_ids = heads_of[:, 0]
    first = jnp.sum(
        (document_ids[None, :] < first_ids[:, None]).astype(jnp.int32), axis=1) // BLOCK
    smem = pl.BlockSpec(memory_space=pltpu.SMEM)
    vmem = pl.BlockSpec(memory_space=pltpu.VMEM)
    heads = log_norm.shape[0]
    return pl.pallas_call(
        grads_kernel,
        out_shape=(
            jax.ShapeDtypeStruct(queries.shape, jnp.float32),
            jax.ShapeDtypeStruct((total, 2 * D_HEAD), sum_type),
        ),
        in_specs=[smem] * 4 + [vmem] * 6,
        out_specs=(vmem, vmem),
        scratch_shapes=[
            pltpu.VMEM((total, 2 * D_HEAD), jnp.float32),
            pltpu.SMEM((blocks,), jnp.int32),
            pltpu.VMEM((D_HEAD, heads * BLOCK), jnp.float32),
        ],
        name="grads",
    )(block_order, first, starts, block_layout.reshape(-1), heads_of,
      queries, out_grad, attn_out, log_norm, kv_all)


def body(
    queries, keys, values, attn_out, out_grad, log_norm, block_layout, document_ids, block_order
):
    rows = keys.shape[0]
    heads = log_norm.shape[0]
    kv_heads = keys.shape[1] // D_HEAD
    repeats = GROUP // heads
    pair = jnp.concatenate(
        [keys.reshape(rows, kv_heads, D_HEAD), values.reshape(rows, kv_heads, D_HEAD)], axis=2)
    pair = jnp.broadcast_to(pair[:, :, None, :], (rows, kv_heads, repeats, 2 * D_HEAD))
    pair = lax.all_to_all(
        pair.reshape(rows, -1), "head", split_axis=1, concat_axis=0, tiled=True)
    kv_all = lax.all_gather(pair, "seq", axis=0, tiled=True)
    dq, dkv = local_grads(queries, out_grad, attn_out, log_norm, kv_all, block_layout,
                          document_ids, block_order, jnp.float32)
    dkv = lax.psum_scatter(dkv, "seq", scatter_dimension=0, tiled=True)
    dkv = lax.all_to_all(dkv, "head", split_axis=0, concat_axis=1, tiled=True)
    dkv = dkv.reshape(rows, kv_heads, repeats, 2, D_HEAD).sum(axis=2)
    return (dq, dkv[:, :, 0].reshape(rows, -1), dkv[:, :, 1].reshape(rows, -1))


def solution(mesh):
    in_specs = (
        P("seq", "head"),
        P(("seq", "head"), None),
        P(("seq", "head"), None),
        P("seq", "head"),
        P("seq", "head"),
        P("head", "seq"),
        P("head", None, None),
        P(),
        P(),
    )
    out_specs = (P("seq", "head"), P(("seq", "head"), None), P(("seq", "head"), None))
    return jax.shard_map(body, mesh=mesh, in_specs=in_specs, out_specs=out_specs, check_vma=False)
```

time: 241 us -> 130 us (0.54)
  local copies, waits for them, and re-layouts: 69.5 us -> 6.19 us
  matrix products: 34.9 us -> 0 us
  starting transfers between devices: 29.3 us -> 0.08 us
  other arithmetic: 30.9 us -> 3.41 us
  blocking collectives: 0 us -> 21.6 us
  between operations: 0.97 us -> 14.1 us
  Pallas kernels: 0 us -> 8.42 us
  waiting for transfers between devices: 72.3 us -> 75.1 us
    ppermute x30 -> x0, waiting for transfers between devices: 61.2 us -> none  [shifted(): return lax.ppermute(value, axis, pairs)]
    reduce_scatter x0 -> x1, waiting for transfers between devices: none -> 51.2 us  [body(): dkv = lax.psum_scatter(dkv, 'seq', scatter_dimension=0, tiled=True)]
    gather x9 -> x0, local copies, waits for them, and re-layouts: 37.3 us -> none  [lookup_rows(): return (position, jnp.take(document_ids, position), placed_hit)]
    dot_general x48 -> x0, matrix products: 34.8 us -> none  [the longest x8 12.6 us: block_grads(): jnp.einsum('qhd,kd->hqk', query_heads, key_block, preferred_element_type=...]
    all_gather x0 -> x1, waiting for transfers between devices: none -> 23.9 us  [body(): kv_all = lax.all_gather(pair, 'seq', axis=0, tiled=True)]
    all_to_all x0 -> x2, blocking collectives: none -> 21.6 us  [the longest x1 10.8 us: body(): lax.all_to_all(pair.reshape(rows, -1), 'head', split_axis=1, concat_axis=...]
    while x85 -> x0, local copies, waits for them, and re-layouts: 21.4 us -> none
    all_to_all x4 -> x0, starting transfers between devices: 16.2 us -> none  [the longest x1 5.19 us: body(): lax.all_to_all(widen(keys), 'head', split_axis=1, concat_axis=0, tiled=True)]
  transfers between devices with their start and end apart: 34 -> 2, of which waited for: 18 -> 2; matrix products, arithmetic and copies ran while one was open for 46% -> 4% of each run, Pallas kernels for 0% -> 0%
where the time goes in v1:
time: 130 us; the launch traced here: 129 us
  waiting for transfers between devices  75.1 us (58%)
  blocking collectives  21.6 us (17%)
  between operations  14.1 us (11%)
  Pallas kernels  8.42 us (6%)
  local copies, waits for them, and re-layouts  6.19 us (5%)
  other arithmetic  3.41 us (3%)
    reduce_scatter x1, waiting for transfers between devices, body(): dkv = lax.psum_scatter(dkv, 'seq', scatter_dimension=0, tiled=True)  51.2 us
    all_gather x1, waiting for transfers between devices, body(): kv_all = lax.all_gather(pair, 'seq', axis=0, tiled=True)  23.9 us
    all_to_all x1, blocking collectives, body(): lax.all_to_all(pair.reshape(rows, -1), 'head', split_axis=1, concat_axis=...  10.8 us
    all_to_all x1, blocking collectives, body(): dkv = lax.all_to_all(dkv, 'head', split_axis=0, concat_axis=1, tiled=True)  10.8 us
    pallas_call x1, Pallas kernels, local_grads(): pl.pallas_call(grads_kernel, out_shape=(jax.ShapeDtypeStruct(queries.shap...  8.42 us
  transfers between devices with their start and end apart: 2, of which 2 were waited for; matrix products, arithmetic and copies ran while one was open for 4% of the time, Pallas kernels for 0%

profile of v1, /device:TPU:0, one launch (start us, length us, event | category | flops | bytes accessed | tf_op | source)
XLA Modules:
  0.0 128.9 jit_solution(14687089434354209287)
XLA Ops:
  7.2 0.0 all-gather.2.cloned.1.call-start
  7.2 0.9 reshape.34
  8.1 0.9 reshape.35
  8.9 0.1 pad_maximum_fusion
  9.1 10.8 %all_to_all.35 = bf16[128,4,256]{2,0,1:T(8,128)(2,1)} all-to-all(bf16[128,4,256]{2,0,1:T(8,128)(2,1)S(1)} %bitcast.13), channel_id=1, replica_groups=mesh['seq'=8,'head'=4] {'head'}, dimensions={1} | all-to-all | bytes 524288 | tf_op jit(solution)/shard_map/all_to_all | solution.py:154
  19.9 0.0 all-gather.2.cloned.1.call-update
  20.0 0.0 reduce-scatter.2.cloned.1.call-start
  20.0 1.4 %reshape.33.layout = s32[2048]{0:T(1024)} reshape(s32[2,32,32]{2,1,0:T(8,128)} %param.15) | data formatting | bytes 16384 | tf_op jit(solution)/shard_map/reshape | solution.py:140
  21.5 0.8 slice_reduce_fusion
  22.3 1.4 %convert_reduce_fusion.1.starts = s32[8]{0:T(128)} fusion(s32[4096]{0:T(1024)} %param.16), kind=kLoop, calls=%fused_computation.2 | loop fusion | flops 98296 | bytes 16416 | tf_op jit(solution)/shard_map/reduce_sum | solution.py:116
  23.7 0.9 convert_reduce_fusion
  24.6 0.5 and_select_fusion.first
  25.1 23.9 %all-gather.2.cloned.1.call-done.kv_ref = bf16[4096,256]{1,0:T(8,128)(2,1)} async-done(((bf16[512,256]{1,0:T(8,128)(2,1)}), bf16[4096,256]{1,0:T(8,128)(2,1)}) %all-gather.2.cloned.1.call-update) | async-done | bytes 2097168 | tf_op jit(solution)/shard_map/all_gather | solution.py:156
  49.0 8.4 %grads.1 = (f32[512,256]{1,0:T(8,128)}, f32[4096,256]{1,0:T(8,128)}) custom-call(s32[32]{0:T(128)} %order.1, s32[32]{0:T(128)} %and_select_fusion.first, s32[8]{0:T(128)} %convert_reduce_fusion.1.starts, s32[2048]{0:T(1024)} %reshape.33.layout, s32[32,128]{1,0:T(8,128)} %bitcast.18, bf16[512,256]{1,0:T(8,128)(2,1)} %q_ref.1, bf16[512,256]{1,0:T(8,128)(2,1)} %do_ref.1, ...), custom_call_target="tpu_custom_call" | custom-call | tf_op jit(solution)/shard_map/grads/pallas_call | solution.py:126
  57.4 0.0 reduce-scatter.2.cloned.1.call-update
  57.4 51.2 %reduce-scatter.2.cloned.1.call-done = f32[512,256]{1,0:T(8,128)} async-done(((f32[4096,256]{1,0:T(8,128)}), f32[512,256]{1,0:T(8,128)}) %reduce-scatter.2.cloned.1.call-update) | async-done | bytes 524304 | tf_op jit(solution)/shard_map/reduce_scatter | solution.py:159
  108.7 10.8 %all_to_all.36 = f32[4,128,256]{2,1,0:T(8,128)S(1)} all-to-all(f32[4,128,256]{2,1,0:T(8,128)} %bitcast.14), channel_id=1, replica_groups=mesh['seq'=8,'head'=4] {'head'}, dimensions={0} | all-to-all | bytes 1048576 | tf_op jit(solution)/shard_map/all_to_all | solution.py:160
  119.4 0.3 reshape.36
  119.7 0.4 reduce_sum.29
  120.1 0.2 fusion
  120.3 0.1 copy.22
  120.4 0.8 copy.24
  121.2 0.1 copy.21
  121.3 0.8 copy.23
  (2 shorter events, 0.0 us)
Async XLA Ops:
  7.2 41.8 %all-gather.2.cloned.1.call-start = ((), (), s32[]{:S(2)}) async-start(), calls=%async_computation.3 | async-start | bytes 2359296 | tf_op jit(solution)/shard_map/all_gather | solution.py:156
  20.0 88.7 %reduce-scatter.2.cloned.1.call-start = ((), (), s32[]{:S(2)}) async-start(), calls=%async_computation.4 | async-start | bytes 4718592 | tf_op jit(solution)/shard_map/reduce_scatter | solution.py:159
Sparse Core Ops, SparseCore 0:
  20.1 28.8 all-gather.1
  57.6 51.0 reduce-scatter.1
